TPU v7x, 256 devices: a 2x2x32 block of a 4x8x32 slice. The times are simulated.
256 devices in a mesh: member: 4 (over y, x), node: 64 (over z, core).
Axes of the slice: x: 2, y: 2, z: 32, core: 2. Of those that a mesh axis runs over, the one named last changes fastest.
The devices are a block of a 4x8x32 slice.
Arguments:
- conditioning: bfloat16 [168, 262144], P(None, ('member', 'node')), parts along dimension 1, may hold values from -6 to 6
- target_state: float32 [84, 262144], P(None, ('member', 'node')), parts along dimension 1, may hold values from -6 to 6
- noise_sample: float32 [84, 262144], P(None, ('member', 'node')), parts along dimension 1, may hold values from -6 to 6
- step_index: int32 [4], P('member'), parts along dimension 0, may hold values from 0 to 19
- mesh_features: float32 [3, 40960], P(None, 'node'), may hold values from -1 to 1
- edge_geometry: float32 [4, 262144], P(None, 'node'), may hold values from -6 to 6
- edge_slot: int32 [262144], P('node'), may hold values from 0 to 1023, as said below
- edge_receiver: int32 [262144], P('node'), may hold values from 0 to 639
- send_rows: int32 [4096, 16], P('node'), may hold values from 0 to 1023
- edge_count: int32 [64], P('node'), may hold values from 1503 to 4096, as said below
- embed_weight: bfloat16 [252, 512], replicated, may hold values from -0.375 to 0.375
- mesh_weight: float32 [3, 512], replicated, may hold values from -3.5 to 3.5
- geom_weight: float32 [4, 512], replicated, may hold values from -3 to 3
- sender_weight: bfloat16 [512, 512], P('node'), may hold values from -0.15625 to 0.15625
- edge_weight: bfloat16 [512, 512], P('node'), may hold values from -0.15625 to 0.15625
- receiver_weight: bfloat16 [512, 512], P('node'), may hold values from -0.15625 to 0.15625
- message_weight: bfloat16 [512, 512], P('node'), may hold values from -0.25 to 0.25
- node_weight: bfloat16 [1024, 512], P('node'), may hold values from -0.1875 to 0.1875
- output_weight: bfloat16 [512, 512], P('node'), may hold values from -0.25 to 0.25
- noise_weight: float32 [32, 512], replicated, may hold values from -1 to 1
- film_weight: bfloat16 [512, 2048], replicated, may hold values from -0.25 to 0.25
Outputs:
- mesh_latent: bfloat16 [40960, 2048], P('node', 'member'), parts along dimension 1
There are 4 independent parts, one for each index of `member`. A program takes and returns all parts, laid end to end along the dimension named above; an argument that names none is the same for every part. Nothing has to cross between parts.
Inputs may be any that keep to these rules, and one draw needn't show every extreme that they name: `edge_slot`: on each device, the live slots name every entry of its 64 * 16 list at least once, or as many distinct entries as there are live slots where these are fewer. `edge_count`: the counts sum to 64 * 2048 and one device has all 4096 slots live.
All inputs are finite; a program needn't handle non-finite values.
Results may differ from a plain program's by a relative error of at most 0.0071.
Values may be sent and summed in bfloat16 or wider, within the bound.
No kernel may reach another device: no remote copies, remote signals or barrier semaphores. Data moves between devices by JAX's collectives and lax.ppermute only.
A program may use at most 64 MiB of HBM per device.

v0:
```python
import functools

import jax
import jax.numpy as jnp
from jax import lax
from jax.experimental import pallas as pl
from jax.experimental.pallas import tpu as pltpu
from jax.sharding import PartitionSpec as P


STEPS = 20

sigma_top = 80.0
sigma_low = 0.03
rho_power = 7.0
norm_eps = 1e-05

NEAR = 4
QUAD = 4

bf16 = jnp.bfloat16
f32 = jnp.float32


def silu(x):
    half = 0.5 * x
    return half + half * jnp.tanh(half)


def node_of(position, far):
    core, rest = divmod(position, NEAR * far)
    near, k = divmod(rest, far)
    return (near + NEAR * k) * 2 + core


def permute_rows(values, far, group):
    return jnp.concatenate(
        [
            values[node_of(p, far) * group : (node_of(p, far) + 1) * group]
            for p in range(2 * NEAR * far)
        ],
        axis=0,
    )


def norm_rows(values):
    mean = jnp.mean(values, axis=0, keepdims=True)
    centred = values - mean
    var = jnp.mean(centred * centred, axis=0, keepdims=True)
    return centred * lax.rsqrt(var + norm_eps)


def pick_kernel(noise_ref, cond_ref, target_ref, sample_ref, rows_ref, out_ref, raw_ref):
    sigma, scale = noise_ref[0], noise_ref[1]
    cond_rows, var_rows = cond_ref.shape[0], target_ref.shape[0]
    total = raw_ref.shape[0]
    raw_ref[total - 8 :, :] = jnp.zeros((8, raw_ref.shape[1]), f32)
    raw_ref[:cond_rows, :] = cond_ref[...].astype(f32)
    noisy = (target_ref[...] + sigma * sample_ref[...]) / scale
    raw_ref[cond_rows : cond_rows + var_rows, :] = noisy
    raw = raw_ref[...].astype(bf16)
    points = raw.shape[1]
    picks = out_ref.shape[0]
    step = min(256, picks)
    for start in range(0, picks, step):
        wanted = rows_ref[:, start : start + step]
        hot = jnp.where(
            lax.broadcasted_iota(jnp.int32, (points, step), 0) == wanted, 1.0, 0.0
        ).astype(bf16)
        got = jnp.dot(raw, hot, preferred_element_type=f32)
        out_ref[start : start + step, :] = got.T.astype(bf16)


def pack_kernel(*refs):
    blocks, out_ref = refs[:-1], refs[-1]
    lanes = out_ref.shape[2]
    quarter = lax.axis_index("member") & (QUAD - 1)
    at = pl.multiple_of(quarter * lanes, lanes)
    rows = jnp.concatenate([b[:, pl.ds(at, lanes)].astype(f32) for b in blocks], axis=0)
    rows = rows.astype(bf16)
    for k in range(out_ref.shape[0]):
        out_ref[k] = rows


def early_kernel(
    far,
    first_w_ref,
    geom_ref,
    mesh_ref,
    recv_ref,
    *refs,
):
    pieces = refs[:8]
    pre_ref, sender_ref, message_ref, node_ref, output_ref, embed_ref = refs[8:14]
    edge_ref, recv_w_ref, proj_ref = refs[14:]
    lanes = pieces[0].shape[-1]
    depth = NEAR * far * 8
    groups = lanes // 8
    ks = groups // 2 // NEAR
    corners = geom_ref.shape[0]

    def first_layer(ref, begin):
        total = 0.0
        for k in range(ref.shape[0]):
            total = total + first_w_ref[:, begin + k : begin + k + 1] * ref[k : k + 1, :]
        return silu(total)

    @pl.when(pl.program_id(0) == 0)
    def _():
        quarter = lax.axis_index("member") & (QUAD - 1)
        node = lax.axis_index("node")
        core = node & 1
        chip = (node >> 1) & (NEAR - 1)
        for number, piece_ref in enumerate(pieces):
            c = core ^ (number // 4)
            mask = (0, 1 + c, 2 - c, 3)[number % 4]
            q = quarter ^ mask
            piece = jnp.concatenate(
                [piece_ref[chip ^ near].astype(f32) for near in range(NEAR)], axis=0
            )
            cols = pl.ds(pl.multiple_of(c * depth, depth), depth)
            wide = pl.ds(pl.multiple_of(c * 2 * depth, 2 * depth), 2 * depth)
            rows = pl.ds(pl.multiple_of(q * lanes, lanes), lanes)

            def turned(first, count):
                return piece[:, first : first + count, :].reshape(-1, lanes).T

            def spread(ref, values, where):
                for c2 in range(2):
                    for near in range(NEAR):
                        block = jnp.concatenate(
                            [
                                values[((near + NEAR * j) * 2 + c2) * 8 :][:8]
                                for j in range(ks)
                            ],
                            axis=0,
                        )
                        at = (c2 * NEAR * far + near * far) * 8 + q * (8 * ks)
                        at = pl.multiple_of(at, 8 * ks)
                        ref[pl.ds(at, 8 * ks), where] = block.astype(bf16)

            spread(sender_ref, turned(0, 8), cols)
            spread(edge_ref, turned(8, 8), cols)
            spread(recv_w_ref, turned(16, 8), cols)
            message_ref[rows, cols] = turned(24, 8).astype(bf16)
            spread(node_ref, turned(32, 16), wide)
            output_ref[rows, cols] = turned(48, 8).astype(bf16)
        embed = first_layer(mesh_ref, corners)
        embed_ref[...] = embed.astype(bf16)
        ordered = permute_rows(embed, far, 8).astype(bf16)
        proj_ref[...] = jnp.dot(
            recv_w_ref[...], ordered, preferred_element_type=f32
        ).astype(bf16)

    edges = geom_ref.shape[1]
    edge_embed = permute_rows(first_layer(geom_ref, 0), far, 8).astype(bf16)
    nodes = proj_ref.shape[1]
    hot = jnp.where(
        lax.broadcasted_iota(jnp.int32, (nodes, edges), 0) == recv_ref[...], 1.0, 0.0
    ).astype(bf16)
    pre = jnp.dot(edge_ref[...], edge_embed, preferred_element_type=f32)
    pre = pre + jnp.dot(proj_ref[...], hot, preferred_element_type=f32)
    pre_ref[0] = pre.astype(bf16)


def late_kernel(
    far,
    count_ref,
    film_ref,
    slot_ref,
    recv_ref,
    arrived_hbm,
    grid_w_hbm,
    sender_hbm,
    pre_hbm,
    message_hbm,
    embed_hbm,
    node_hbm,
    output_hbm,
    out_ref,
    arrived_ref,
    grid_w_ref,
    sender_ref,
    pre_ref,
    message_ref,
    embed_ref,
    node_ref,
    output_ref,
    table_ref,
    total_ref,
    sems,
    pre_sems,
):
    count = count_ref[0]
    steps, _, edges = pre_ref.shape
    whole = [
        pltpu.make_async_copy(src, dst, sems.at[k])
        for k, (src, dst) in enumerate(
            (
                (arrived_hbm, arrived_ref),
                (grid_w_hbm, grid_w_ref),
                (sender_hbm, sender_ref),
                (message_hbm, message_ref),
                (embed_hbm, embed_ref),
                (node_hbm, node_ref),
                (output_hbm, output_ref),
            )
        )
    ]

    def part(k):
        return pltpu.make_async_copy(pre_hbm.at[k], pre_ref.at[k], pre_sems.at[k])

    for copy in whole[:4]:
        copy.start()
    for k in range(steps):
        part(k).start()
    for copy in whole[4:]:
        copy.start()

    total_ref[...] = jnp.zeros_like(total_ref)
    whole[0].wait()
    whole[1].wait()
    latent = silu(
        lax.dot_general(
            grid_w_ref[...],
            arrived_ref[...],
            (((1,), (1,)), ((), ())),
            preferred_element_type=f32,
        )
    )
    ordered = permute_rows(latent, far, 8).astype(bf16)
    whole[2].wait()
    table_ref[...] = jnp.dot(sender_ref[...], ordered, preferred_element_type=f32).astype(bf16)
    whole[3].wait()

    listed = table_ref.shape[1]
    nodes = total_ref.shape[1]

    def add_block(k, carry):
        start = k * edges
        lanes = pl.ds(pl.multiple_of(start, edges), edges)
        hot = jnp.where(
            lax.broadcasted_iota(jnp.int32, (listed, edges), 0) == slot_ref[:, lanes], 1.0, 0.0
        ).astype(bf16)
        pre = pre_ref[k].astype(f32)
        pre = pre + jnp.dot(table_ref[...], hot, preferred_element_type=f32)
        hidden = silu(pre).astype(bf16)
        mixed = jnp.dot(message_ref[...], hidden, preferred_element_type=f32)
        message = norm_rows(mixed) * film_ref[:, 0:1] + film_ref[:, 1:2]
        message = message.astype(bf16)
        live = start + lax.broadcasted_iota(jnp.int32, (1, edges), 1) < count
        target = jnp.where(live, recv_ref[:, lanes], -1)
        home = jnp.where(
            lax.broadcasted_iota(jnp.int32, (nodes, edges), 0) == target, 1.0, 0.0
        ).astype(bf16)
        total_ref[...] += lax.dot_general(
            message, home, (((1,), (1,)), ((), ())), preferred_element_type=f32
        )
        return carry

    live_blocks = (count + edges - 1) // edges
    for k in range(steps):
        part(k).wait()
    lax.fori_loop(0, live_blocks, add_block, 0)
    for copy in whole[4:]:
        copy.wait()
    embed = embed_ref[...]
    joined = jnp.concatenate([embed, total_ref[...].astype(bf16)], axis=0)
    ordered = permute_rows(joined, far, 16)
    update = silu(jnp.dot(node_ref[...], ordered, preferred_element_type=f32)).astype(bf16)
    result = jnp.dot(output_ref[...], update, preferred_element_type=f32)
    latent = embed.astype(f32) + norm_rows(result) * film_ref[:, 2:3] + film_ref[:, 3:4]
    out_ref[...] = latent.T.astype(bf16)


def gather_weights(blocks, members, nodes):
    rows = sum(b.shape[0] for b in blocks)
    lanes = blocks[0].shape[1] // QUAD
    far = nodes // 2 // NEAR
    strided = [
        [(a + NEAR * k) * 2 + c for k in range(far)] for a in range(NEAR) for c in range(2)
    ]
    in_vmem = pl.BlockSpec(memory_space=pltpu.VMEM)
    held = pl.pallas_call(
        pack_kernel,
        out_shape=jax.ShapeDtypeStruct((far, rows, lanes), bf16),
        in_specs=[in_vmem] * len(blocks),
        out_specs=in_vmem,
        name="pack",
    )(*blocks)
    held = lax.all_to_all(held, "node", 0, 0, tiled=True, axis_index_groups=strided)
    near = [
        lax.ppermute(held, "node", [(n, n ^ (2 * j)) for n in range(nodes)])
        for j in range(1, NEAR)
    ]
    held = jnp.stack([held] + near)

    def swap(values, even, odd):
        pairs = [
            (m * nodes + n, (m ^ (odd if n % 2 else even)) * nodes + n)
            for m in range(members)
            for n in range(nodes)
        ]
        return lax.ppermute(values, ("member", "node"), pairs)

    first = swap(held, 1, 2)
    second = swap(held, 2, 1)
    third = swap(first, 2, 1)
    own = [held, first, second, third]
    pairs = [(n, n ^ 1) for n in range(nodes)]
    return own + [lax.ppermute(piece, "node", pairs) for piece in own]


def vmem(shape, index=None):
    if index is None:
        return pl.BlockSpec(shape, lambda i: (0,) * len(shape))
    return pl.BlockSpec(shape, index)


def per_device(
    members,
    nodes,
    conditioning,
    target_state,
    noise_sample,
    step_index,
    mesh_features,
    edge_geometry,
    edge_slot,
    edge_receiver,
    send_rows,
    edge_count,
    embed_weight,
    mesh_weight,
    geom_weight,
    sender_weight,
    edge_weight,
    receiver_weight,
    message_weight,
    node_weight,
    output_weight,
    noise_weight,
    film_weight,
):
    width = embed_weight.shape[1]
    chips = nodes // 2
    far = chips // NEAR
    blocks = [
        sender_weight, edge_weight, receiver_weight, message_weight, node_weight, output_weight
    ]
    freqs = noise_weight.shape[0] // 2
    frac = step_index[0].astype(f32) / (STEPS - 1)
    upper = sigma_top ** (1.0 / rho_power)
    lower = sigma_low ** (1.0 / rho_power)
    sigma = (upper + frac * (lower - upper)) ** rho_power
    noise = jnp.stack([sigma, jnp.sqrt(sigma * sigma + 1.0)])

    picks = send_rows.size
    raw_rows = conditioning.shape[0] + target_state.shape[0]
    padded = raw_rows + -raw_rows % 16
    points = conditioning.shape[1]
    outgoing = pl.pallas_call(
        pick_kernel,
        out_shape=jax.ShapeDtypeStruct((picks, padded), bf16),
        in_specs=[pl.BlockSpec(memory_space=pltpu.SMEM)]
        + [pl.BlockSpec(memory_space=pltpu.VMEM)] * 4,
        out_specs=pl.BlockSpec(memory_space=pltpu.VMEM),
        scratch_shapes=[pltpu.VMEM((padded, points), f32)],
        cost_estimate=pl.CostEstimate(
            flops=2 * picks * points * padded, bytes_accessed=4 * picks * padded, transcendentals=0
        ),
        name="pick_rows",
    )(noise, conditioning, target_state, noise_sample, send_rows.reshape(1, picks))
    weights = gather_weights(blocks, members, nodes)
    arrived = lax.all_to_all(
        outgoing.reshape(nodes, picks // nodes, padded), "node", 0, 0, tiled=True
    ).reshape(picks, padded)

    angle = 0.25 * jnp.log(sigma) * (jnp.arange(freqs, dtype=f32) + 1.0)
    fourier = jnp.concatenate([jnp.sin(angle), jnp.cos(angle)])[None, :]
    cond = jax.nn.silu(jnp.dot(fourier, noise_weight, precision=lax.Precision.HIGHEST)).astype(bf16)
    film = jnp.dot(cond, film_weight, preferred_element_type=f32).reshape(4, width)
    film = (film + jnp.array([1.0, 0.0, 1.0, 0.0], f32)[:, None]).T

    first_w = jnp.concatenate([geom_weight, mesh_weight], axis=0).T
    grid_w = jnp.pad(embed_weight.T, ((0, 0), (0, padded - raw_rows)))

    edges = edge_slot.shape[0]
    mesh_count = mesh_features.shape[1]
    step = min(512, edges)
    steps = edges // step
    slots = edge_slot.reshape(1, edges)
    receivers = edge_receiver.reshape(1, edges)
    smem = pl.BlockSpec(memory_space=pltpu.SMEM)
    lane_block = lambda i: (0, i)

    square = jax.ShapeDtypeStruct((width, width), bf16)
    pre, sender_t, message_t, node_t, output_t, mesh_embed = pl.pallas_call(
        functools.partial(early_kernel, far),
        grid=(steps,),
        out_shape=(
            jax.ShapeDtypeStruct((steps, width, step), bf16),
            square,
            square,
            jax.ShapeDtypeStruct((width, 2 * width), bf16),
            square,
            jax.ShapeDtypeStruct((width, mesh_count), bf16),
        ),
        in_specs=[
            vmem(first_w.shape),
            vmem((edge_geometry.shape[0], step), lane_block),
            vmem(mesh_features.shape),
            vmem((1, step), lane_block),
        ]
        + [vmem(piece.shape) for piece in weights],
        out_specs=(
            vmem((1, width, step), lambda i: (i, 0, 0)),
            vmem((width, width)),
            vmem((width, width)),
            vmem((width, 2 * width)),
            vmem((width, width)),
            vmem((width, mesh_count)),
        ),
        scratch_shapes=[
            pltpu.VMEM((width, width), bf16),
            pltpu.VMEM((width, width), bf16),
            pltpu.VMEM((width, mesh_count), bf16),
        ],
        cost_estimate=pl.CostEstimate(
            flops=2 * edges * width * (width + mesh_count + 256),
            bytes_accessed=2 * edges * width + 64 * weights[0].size,
            transcendentals=edges * width,
        ),
        name="early",
    )(first_w, edge_geometry, mesh_features, receivers, *weights)

    in_vmem = pl.BlockSpec(memory_space=pltpu.VMEM)
    operands = (arrived, grid_w, sender_t, pre, message_t, mesh_embed, node_t, output_t)
    return pl.pallas_call(
        functools.partial(late_kernel, far),
        out_shape=jax.ShapeDtypeStruct((mesh_count, width), bf16),
        in_specs=[smem] + [in_vmem] * 3 + [pl.BlockSpec(memory_space=pl.ANY)] * len(operands),
        out_specs=in_vmem,
        scratch_shapes=[pltpu.VMEM(x.shape, x.dtype) for x in operands]
        + [
            pltpu.VMEM((width, picks), bf16),
            pltpu.VMEM((width, mesh_count), f32),
            pltpu.SemaphoreType.DMA((len(operands) - 1,)),
            pltpu.SemaphoreType.DMA((steps,)),
        ],
        cost_estimate=pl.CostEstimate(
            flops=2 * edges * width * (width + mesh_count + picks),
            bytes_accessed=2 * edges * width,
            transcendentals=edges * width,
        ),
        compiler_params=pltpu.CompilerParams(vmem_limit_bytes=59 << 20),
        name="late",
    )(edge_count, film, slots, receivers, *operands)


def solution(mesh):
    placed = (
        P(None, ("member", "node")),
        P(None, ("member", "node")),
        P(None, ("member", "node")),
        P("member"),
        P(None, "node"),
        P(None, "node"),
        P("node"),
        P("node"),
        P("node", None),
        P("node"),
        P(),
        P(),
        P(),
        P("node", None),
        P("node", None),
        P("node", None),
        P("node", None),
        P("node", None),
        P("node", None),
        P(),
        P(),
    )

    def body(*args):
        return per_device(mesh.shape["member"], mesh.shape["node"], *args)

    return jax.shard_map(
        body, mesh=mesh, in_specs=placed, out_specs=P("node", "member"), check_vma=False
    )
```

profile of v0, /device:TPU:46, one launch (start us, length us, event | category | flops | bytes accessed | tf_op | source)
XLA Modules:
  0.0 178.0 jit_solution(4278240601540697677)
XLA Ops:
  0.0 0.0 copy-start
  0.0 1.5 pack.1
  1.5 0.0 copy-start.5
  1.5 0.0 copy-start.6
  1.5 31.7 %all-to-all-start.1 = ((bf16[8,56,128]{2,1,0:T(8,128)(2,1)}), bf16[8,56,128]{2,1,0:T(8,128)(2,1)S(1)}, u32[]{:S(2)}, u32[]{:S(2)}) async-start(bf16[8,56,128]{2,1,0:T(8,128)(2,1)} %pack.1), calls=%async_computation.1 | async-start | bytes 229376 | tf_op jit(solution)/shard_map/all_to_all | solution.py:292
  33.9 0.8 copy.31
  34.7 0.7 reshape.42.rows_ref
  35.4 0.7 pad_maximum_fusion.2.noise_ref
  36.1 0.0 copy-start.1
  36.1 3.0 %pick_rows.1 = bf16[1024,256]{1,0:T(8,128)(2,1)} custom-call(f32[2]{0:T(128)} %pad_maximum_fusion.2.noise_ref, bf16[168,1024]{1,0:T(8,128)(2,1)} %cond_ref.1, f32[84,1024]{1,0:T(8,128)} %target_ref.1, f32[84,1024]{1,0:T(8,128)} %sample_ref.1, s32[1,1024]{1,0:T(1,128)} %reshape.42.rows_ref), custom_call_target="tpu_custom_call" | custom-call | flops 536870912 | bytes 1048576 | tf_op jit(solution)/shard_map/pick_rows/pallas_call | solution.py:363
  39.1 21.8 %all-to-all-done.1 = bf16[8,56,128]{2,1,0:T(8,128)(2,1)S(1)} async-done(((bf16[8,56,128]{2,1,0:T(8,128)(2,1)}), bf16[8,56,128]{2,1,0:T(8,128)(2,1)S(1)}, u32[]{:S(2)}, u32[]{:S(2)}) %all-to-all-start.1) | async-done | bytes 114720 | tf_op jit(solution)/shard_map/all_to_all | solution.py:292
  60.9 7.4 %all-to-all-start = ((bf16[64,16,256]{2,1,0:T(8,128)(2,1)}), bf16[64,16,256]{2,1,0:T(8,128)(2,1)S(1)}, u32[]{:S(2)}, u32[]{:S(2)}) async-start(bf16[64,16,256]{2,1,0:T(8,128)(2,1)} %bitcast.30), calls=%async_computation | async-start | bytes 1048576 | tf_op jit(solution)/shard_map/all_to_all | solution.py:376
  68.3 0.0 copy-start.4
  68.3 1.2 collective-permute-start
  69.5 2.0 %collective-permute-start.1 = (bf16[8,56,128]{2,1,0:T(8,128)(2,1)S(1)}, bf16[8,56,128]{2,1,0:T(8,128)(2,1)S(1)}, u32[]{:S(2)}, u32[]{:S(2)}) collective-permute-start(bf16[8,56,128]{2,1,0:T(8,128)(2,1)S(1)} %all-to-all-done.1), channel_id=1, source_target_pairs={{0,4},{1,5},{2,6},{3,7},{4,0},{5,1},{6,2},{7,3},{8,12},{9,13},{10,... | collective-permute-start | bytes 344072 | tf_op jit(solution)/shard_map/ppermute | solution.py:294
  71.5 1.3 collective-permute-start.2
  72.8 45.4 %collective-permute-done = bf16[8,56,128]{2,1,0:T(8,128)(2,1)S(1)} collective-permute-done((bf16[8,56,128]{2,1,0:T(8,128)(2,1)S(1)}, bf16[8,56,128]{2,1,0:T(8,128)(2,1)S(1)}, u32[]{:S(2)}, u32[]{:S(2)}) %collective-permute-start) | collective-permute-done | bytes 114720 | tf_op jit(solution)/shard_map/ppermute | solution.py:294
  118.2 0.0 collective-permute-done.1
  118.2 4.5 %collective-permute-done.2 = bf16[8,56,128]{2,1,0:T(8,128)(2,1)S(1)} collective-permute-done((bf16[8,56,128]{2,1,0:T(8,128)(2,1)S(1)}, bf16[8,56,128]{2,1,0:T(8,128)(2,1)S(1)}, u32[]{:S(2)}, u32[]{:S(2)}) %collective-permute-start.2) | collective-permute-done | bytes 114720 | tf_op jit(solution)/shard_map/ppermute | solution.py:294
  122.7 0.1 pad_maximum_fusion.refs_0_
  122.8 0.0 copy-start.3
  122.8 0.0 copy-start.7
  122.8 0.5 collective-permute-start.3
  123.4 0.0 copy-done.5
  123.4 0.0 copy-done.6
  123.4 0.4 collective-permute-start.4
  123.8 11.3 %collective-permute-done.3.refs_1_ = bf16[4,8,56,128]{3,2,1,0:T(8,128)(2,1)} collective-permute-done((bf16[4,8,56,128]{3,2,1,0:T(8,128)(2,1)S(1)}, bf16[4,8,56,128]{3,2,1,0:T(8,128)(2,1)}, u32[]{:S(2)}, u32[]{:S(2)}) %collective-permute-start.3) | collective-permute-done | bytes 458784 | tf_op jit(solution)/shard_map/ppermute | solution.py:305
  135.1 1.5 collective-permute-start.5
  136.6 0.9 copy.33
  137.5 0.0 copy-done
  137.5 0.2 fusion.5
  137.7 0.1 collective-permute-start.6
  137.9 0.5 collective-permute-start.7
  138.3 0.0 collective-permute-done.4.refs_2_
  138.3 0.2 collective-permute-start.8
  138.5 5.4 %collective-permute-done.5.refs_3_ = bf16[4,8,56,128]{3,2,1,0:T(8,128)(2,1)} collective-permute-done((bf16[4,8,56,128]{3,2,1,0:T(8,128)(2,1)}, bf16[4,8,56,128]{3,2,1,0:T(8,128)(2,1)}, u32[]{:S(2)}, u32[]{:S(2)}) %collective-permute-start.5) | collective-permute-done | bytes 458784 | tf_op jit(solution)/shard_map/ppermute | solution.py:305
  143.9 0.0 collective-permute-start.9
  143.9 0.0 copy-done.1
  143.9 0.4 fusion
  144.3 0.2 copy.35
  144.4 0.0 copy-done.4
  144.4 0.1 copy.32
  145.2 0.7 pad.4.grid_w_hbm
  145.9 0.0 copy-done.7
  146.0 0.7 fusion.3.film_ref
  146.7 0.0 copy-done.3
  146.7 0.0 collective-permute-done.6.refs_4_
  146.7 0.0 collective-permute-done.7.refs_5_
  146.7 0.0 collective-permute-done.8.refs_6_
  146.7 0.0 collective-permute-done.9.refs_7_
  146.7 13.6 %early.1 = (bf16[8,512,512]{2,1,0:T(8,128)(2,1)}, bf16[512,512]{1,0:T(8,128)(2,1)}, bf16[512,512]{1,0:T(8,128)(2,1)}, bf16[512,1024]{1,0:T(8,128)(2,1)}, bf16[51...) custom-call(f32[512,7]{1,0:T(8,128)} %bitcast.33, f32[4,4096]{1,0:T(4,128)} %geom_ref.1, f32[3,640]{1,0:T(4,128)} %mesh_ref.1, ...), custom_call_target="tpu_custom_call" | custom-call | flops 5905580032 | bytes 18874368 | tf_op jit(solution)/shard_map/early/pallas_call | solution.py:399
  160.3 0.0 all-to-all-done
  160.3 0.0 copy-start.2
  160.3 0.8 copy-done.2
  161.1 16.8 %late.1 = bf16[640,512]{1,0:T(8,128)(2,1)} custom-call(s32[1]{0:T(128)S(6)} %copy.42.count_ref, f32[512,4]{1,0:T(8,128)} %fusion.3.film_ref, s32[1,4096]{1,0:T(1,128)} %bitcast.38, s32[1,4096]{1,0:T(1,128)} %bitcast.40, bf16[1024,256]{1,0:T(8,128)(2,1)} %bitcast.31, bf16[512,256]{1,0:T(8,128)(2,1)} %pad.4.grid_w_hbm, ...), custom_call_target="tpu_custom_call" | custom-call | flops 9126805504 | bytes 4194304 | tf_op jit(solution)/shard_map/late/pallas_call | solution.py:440
  (4 shorter events, 0.1 us)
Async XLA Ops:
  0.0 137.5 %copy-start = (f32[32,512]{1,0:T(8,128)S(1)}, f32[32,512]{1,0:T(8,128)}, u32[]{:S(2)}) copy-start(f32[32,512]{1,0:T(8,128)} %param.41) | copy-start | bytes 196612
  1.5 121.9 %copy-start.5 = (f32[3,512]{1,0:T(4,128)S(1)}, f32[3,512]{1,0:T(4,128)}, u32[]{:S(2)}) copy-start(f32[3,512]{1,0:T(4,128)} %param.33) | copy-start | bytes 18436
  1.5 121.9 %copy-start.6 = (f32[4,512]{1,0:T(4,128)S(1)}, f32[4,512]{1,0:T(4,128)}, u32[]{:S(2)}) copy-start(f32[4,512]{1,0:T(4,128)} %param.34) | copy-start | bytes 24580
  1.5 59.4 %all-to-all-start.1 = ((bf16[8,56,128]{2,1,0:T(8,128)(2,1)}), bf16[8,56,128]{2,1,0:T(8,128)(2,1)S(1)}, u32[]{:S(2)}, u32[]{:S(2)}) async-start(bf16[8,56,128]{2,1,0:T(8,128)(2,1)} %pack.1), calls=%async_computation.1 | async-start | bytes 229376 | tf_op jit(solution)/shard_map/all_to_all | solution.py:292
  36.1 107.8 %copy-start.1 = (bf16[512,2048]{1,0:T(8,128)(2,1)S(1)}, bf16[512,2048]{1,0:T(8,128)(2,1)}, u32[]{:S(2)}) copy-start(bf16[512,2048]{1,0:T(8,128)(2,1)} %param.42) | copy-start | bytes 6291460
  60.9 99.4 %all-to-all-start = ((bf16[64,16,256]{2,1,0:T(8,128)(2,1)}), bf16[64,16,256]{2,1,0:T(8,128)(2,1)S(1)}, u32[]{:S(2)}, u32[]{:S(2)}) async-start(bf16[64,16,256]{2,1,0:T(8,128)(2,1)} %bitcast.30), calls=%async_computation | async-start | bytes 1048576 | tf_op jit(solution)/shard_map/all_to_all | solution.py:376
  68.3 76.1 %copy-start.4 = (bf16[252,512]{1,0:T(8,128)(2,1)S(1)}, bf16[252,512]{1,0:T(8,128)(2,1)}, u32[]{:S(2)}) copy-start(bf16[252,512]{1,0:T(8,128)(2,1)} %param.32) | copy-start | bytes 774148
  68.3 49.9 %collective-permute-start = (bf16[8,56,128]{2,1,0:T(8,128)(2,1)S(1)}, bf16[8,56,128]{2,1,0:T(8,128)(2,1)S(1)}, u32[]{:S(2)}, u32[]{:S(2)}) collective-permute-start(bf16[8,56,128]{2,1,0:T(8,128)(2,1)S(1)} %all-to-all-done.1), channel_id=1, source_target_pairs={{0,2},{1,3},{2,0},{3,1},{4,6},{5,7},{6,4},{7,5},{8,10},{9,11},{10,... | collective-permute-start | bytes 344072 | tf_op jit(solution)/shard_map/ppermute | solution.py:294
  69.5 48.8 %collective-permute-start.1 = (bf16[8,56,128]{2,1,0:T(8,128)(2,1)S(1)}, bf16[8,56,128]{2,1,0:T(8,128)(2,1)S(1)}, u32[]{:S(2)}, u32[]{:S(2)}) collective-permute-start(bf16[8,56,128]{2,1,0:T(8,128)(2,1)S(1)} %all-to-all-done.1), channel_id=1, source_target_pairs={{0,4},{1,5},{2,6},{3,7},{4,0},{5,1},{6,2},{7,3},{8,12},{9,13},{10,... | collective-permute-start | bytes 344072 | tf_op jit(solution)/shard_map/ppermute | solution.py:294
  71.5 51.2 %collective-permute-start.2 = (bf16[8,56,128]{2,1,0:T(8,128)(2,1)S(1)}, bf16[8,56,128]{2,1,0:T(8,128)(2,1)S(1)}, u32[]{:S(2)}, u32[]{:S(2)}) collective-permute-start(bf16[8,56,128]{2,1,0:T(8,128)(2,1)S(1)} %all-to-all-done.1), channel_id=1, source_target_pairs={{0,6},{1,7},{2,4},{3,5},{4,2},{5,3},{6,0},{7,1},{8,14},{9,15},{10,... | collective-permute-start | bytes 344072 | tf_op jit(solution)/shard_map/ppermute | solution.py:294
  122.8 23.9 %copy-start.3 = (bf16[4,8,56,128]{3,2,1,0:T(8,128)(2,1)}, bf16[4,8,56,128]{3,2,1,0:T(8,128)(2,1)S(1)}, u32[]{:S(2)}) copy-start(bf16[4,8,56,128]{3,2,1,0:T(8,128)(2,1)S(1)} %pad_maximum_fusion.refs_0_) | copy-start | bytes 1376260
  122.8 23.1 %copy-start.7 = (f32[4]{0:T(128)S(1)}, f32[4]{0:T(128)}, u32[]{:S(2)}) copy-start(f32[4]{0:T(128)} %constant.28.clone) | copy-start | bytes 52
  122.8 12.3 %collective-permute-start.3 = (bf16[4,8,56,128]{3,2,1,0:T(8,128)(2,1)S(1)}, bf16[4,8,56,128]{3,2,1,0:T(8,128)(2,1)}, u32[]{:S(2)}, u32[]{:S(2)}) collective-permute-start(bf16[4,8,56,128]{3,2,1,0:T(8,128)(2,1)S(1)} %pad_maximum_fusion.refs_0_), channel_id=1, source_target_pairs={{0,64},{1,129},{2,66},{3,131},{4,68},{5,133},{6,70},{7,135},{8,72}... | collective-permute-start | bytes 1376264 | tf_op jit(solution)/shard_map/ppermute | solution.py:305
  123.4 14.9 %collective-permute-start.4 = (bf16[4,8,56,128]{3,2,1,0:T(8,128)(2,1)S(1)}, bf16[4,8,56,128]{3,2,1,0:T(8,128)(2,1)}, u32[]{:S(2)}, u32[]{:S(2)}) collective-permute-start(bf16[4,8,56,128]{3,2,1,0:T(8,128)(2,1)S(1)} %pad_maximum_fusion.refs_0_), channel_id=1, source_target_pairs={{0,128},{1,65},{2,130},{3,67},{4,132},{5,69},{6,134},{7,71},{8,136... | collective-permute-start | bytes 1376264 | tf_op jit(solution)/shard_map/ppermute | solution.py:305
  135.1 8.8 %collective-permute-start.5 = (bf16[4,8,56,128]{3,2,1,0:T(8,128)(2,1)}, bf16[4,8,56,128]{3,2,1,0:T(8,128)(2,1)}, u32[]{:S(2)}, u32[]{:S(2)}) collective-permute-start(bf16[4,8,56,128]{3,2,1,0:T(8,128)(2,1)} %collective-permute-done.3.refs_1_), channel_id=1, source_target_pairs={{0,128},{1,65},{2,130},{3,67},{4,132},{5,69},{6,134},{7,71},{8,136... | collective-permute-start | bytes 1376264 | tf_op jit(solution)/shard_map/ppermute | solution.py:305
  137.7 9.0 %collective-permute-start.6 = (bf16[4,8,56,128]{3,2,1,0:T(8,128)(2,1)S(1)}, bf16[4,8,56,128]{3,2,1,0:T(8,128)(2,1)}, u32[]{:S(2)}, u32[]{:S(2)}) collective-permute-start(bf16[4,8,56,128]{3,2,1,0:T(8,128)(2,1)S(1)} %pad_maximum_fusion.refs_0_), channel_id=1, source_target_pairs={{0,1},{1,0},{2,3},{3,2},{4,5},{5,4},{6,7},{7,6},{8,9},{9,8},{10,11... | collective-permute-start | bytes 1376264 | tf_op jit(solution)/shard_map/ppermute | solution.py:312
  137.9 8.8 %collective-permute-start.7 = (bf16[4,8,56,128]{3,2,1,0:T(8,128)(2,1)}, bf16[4,8,56,128]{3,2,1,0:T(8,128)(2,1)}, u32[]{:S(2)}, u32[]{:S(2)}) collective-permute-start(bf16[4,8,56,128]{3,2,1,0:T(8,128)(2,1)} %collective-permute-done.3.refs_1_), channel_id=1, source_target_pairs={{0,1},{1,0},{2,3},{3,2},{4,5},{5,4},{6,7},{7,6},{8,9},{9,8},{10,11... | collective-permute-start | bytes 1376264 | tf_op jit(solution)/shard_map/ppermute | solution.py:312
  138.3 8.3 %collective-permute-start.8 = (bf16[4,8,56,128]{3,2,1,0:T(8,128)(2,1)}, bf16[4,8,56,128]{3,2,1,0:T(8,128)(2,1)}, u32[]{:S(2)}, u32[]{:S(2)}) collective-permute-start(bf16[4,8,56,128]{3,2,1,0:T(8,128)(2,1)} %collective-permute-done.4.refs_2_), channel_id=1, source_target_pairs={{0,1},{1,0},{2,3},{3,2},{4,5},{5,4},{6,7},{7,6},{8,9},{9,8},{10,11... | collective-permute-start | bytes 1376264 | tf_op jit(solution)/shard_map/ppermute | solution.py:312
  143.9 2.8 %collective-permute-start.9 = (bf16[4,8,56,128]{3,2,1,0:T(8,128)(2,1)}, bf16[4,8,56,128]{3,2,1,0:T(8,128)(2,1)}, u32[]{:S(2)}, u32[]{:S(2)}) collective-permute-start(bf16[4,8,56,128]{3,2,1,0:T(8,128)(2,1)} %collective-permute-done.5.refs_3_), channel_id=1, source_target_pairs={{0,1},{1,0},{2,3},{3,2},{4,5},{5,4},{6,7},{7,6},{8,9},{9,8},{10,11... | collective-permute-start | bytes 1376264 | tf_op jit(solution)/shard_map/ppermute | solution.py:312
  160.3 0.8 copy-start.2
where the time goes:
time: 181 us; the launch traced here: 178 us
  waiting for transfers between devices  88.4 us (49%)
  starting transfers between devices  46.8 us (26%)
  Pallas kernels  34.9 us (19%)
  local copies, waits for them, and re-layouts  4.18 us (2%)
    ppermute x3, waiting for transfers between devices, gather_weights(): lax.ppermute(held, 'node', [(n, n ^ 2 * j) for n in range(nodes)])  49.9 us
    all_to_all x1, starting transfers between devices, gather_weights(): lax.all_to_all(held, 'node', 0, 0, tiled=True, axis_index_groups=strided)  31.7 us
    all_to_all x1, waiting for transfers between devices, gather_weights(): lax.all_to_all(held, 'node', 0, 0, tiled=True, axis_index_groups=strided)  21.8 us
    pallas_call x1, Pallas kernels, per_device(): pl.pallas_call(functools.partial(late_kernel, far), out_shape=jax.ShapeDt...  16.8 us
    ppermute x3, waiting for transfers between devices, swap(): return lax.ppermute(values, ('member', 'node'), pairs)  16.7 us
    pallas_call x1, Pallas kernels, per_device(): pl.pallas_call(functools.partial(early_kernel, far), grid=(steps,), out_s...  13.6 us
    all_to_all x1, starting transfers between devices, per_device(): lax.all_to_all(outgoing.reshape(nodes, picks // nodes, padded), 'node', 0...  7.39 us
    ppermute x3, starting transfers between devices, gather_weights(): lax.ppermute(held, 'node', [(n, n ^ 2 * j) for n in range(nodes)])  4.51 us
  transfers between devices with their start and end apart: 12, of which 5 were waited for; matrix products, arithmetic and copies ran while one was open for 3% of the time, Pallas kernels for 9%

commit v1 on v0

--- a/solution.py
+++ b/solution.py
@@ -16,6 +16,7 @@
 norm_eps = 1e-05
 
 NEAR = 4
+EDGE_BLOCK = 1024
 QUAD = 4
 
 bf16 = jnp.bfloat16
@@ -41,6 +42,20 @@
         ],
         axis=0,
     )
+
+
+def one_hot(index, count):
+    low = (index & 255).astype(bf16)
+    high = index >> 8
+    row = lax.broadcasted_iota(jnp.int32, (256, index.shape[1]), 0).astype(bf16)
+    groups = []
+    for g in range(-(-count // 256)):
+        mine = jnp.where(high == g, low, jnp.asarray(-1.0, bf16))
+        rows = min(256, count - 256 * g)
+        groups.append(
+            jnp.where(row[:rows] == mine, jnp.asarray(1.0, bf16), jnp.asarray(0.0, bf16))
+        )
+    return jnp.concatenate(groups, axis=0)
 
 
 def norm_rows(values):
@@ -82,6 +97,18 @@
         out_ref[k] = rows
 
 
+def stored(ref, mesh_count):
+    width = ref.shape[1]
+    first, second, mesh = pl.ds(0, width), pl.ds(width, width), pl.ds(0, mesh_count)
+    return (
+        ref.at[0, :, first],
+        ref.at[0, :, second],
+        ref.at[1],
+        ref.at[2, :, first],
+        ref.at[3, :, mesh],
+    )
+
+
 def early_kernel(
     far,
     first_w_ref,
@@ -91,8 +118,10 @@
     *refs,
 ):
     pieces = refs[:8]
-    pre_ref, sender_ref, message_ref, node_ref, output_ref, embed_ref = refs[8:14]
-    edge_ref, recv_w_ref, proj_ref = refs[14:]
+    pre_ref, store_ref, edge_ref, recv_w_ref, proj_ref = refs[8:]
+    sender_ref, message_ref, node_ref, output_ref, embed_ref = stored(
+        store_ref, mesh_ref.shape[1]
+    )
     lanes = pieces[0].shape[-1]
     depth = NEAR * far * 8
     groups = lanes // 8
@@ -171,12 +200,8 @@
     recv_ref,
     arrived_hbm,
     grid_w_hbm,
-    sender_hbm,
     pre_hbm,
-    message_hbm,
-    embed_hbm,
-    node_hbm,
-    output_hbm,
+    kept_hbm,
     out_ref,
     arrived_ref,
     grid_w_ref,
@@ -193,6 +218,9 @@
 ):
     count = count_ref[0]
     steps, _, edges = pre_ref.shape
+    sender_hbm, message_hbm, node_hbm, output_hbm, embed_hbm = stored(
+        kept_hbm, total_ref.shape[1]
+    )
     whole = [
         pltpu.make_async_copy(src, dst, sems.at[k])
         for k, (src, dst) in enumerate(
@@ -238,11 +266,10 @@
     nodes = total_ref.shape[1]
 
     def add_block(k, carry):
+        part(k).wait()
         start = k * edges
         lanes = pl.ds(pl.multiple_of(start, edges), edges)
-        hot = jnp.where(
-            lax.broadcasted_iota(jnp.int32, (listed, edges), 0) == slot_ref[:, lanes], 1.0, 0.0
-        ).astype(bf16)
+        hot = one_hot(slot_ref[:, lanes], listed)
         pre = pre_ref[k].astype(f32)
         pre = pre + jnp.dot(table_ref[...], hot, preferred_element_type=f32)
         hidden = silu(pre).astype(bf16)
@@ -251,18 +278,20 @@
         message = message.astype(bf16)
         live = start + lax.broadcasted_iota(jnp.int32, (1, edges), 1) < count
         target = jnp.where(live, recv_ref[:, lanes], -1)
-        home = jnp.where(
-            lax.broadcasted_iota(jnp.int32, (nodes, edges), 0) == target, 1.0, 0.0
-        ).astype(bf16)
+        home = one_hot(target, nodes)
         total_ref[...] += lax.dot_general(
             message, home, (((1,), (1,)), ((), ())), preferred_element_type=f32
         )
         return carry
 
     live_blocks = (count + edges - 1) // edges
-    for k in range(steps):
+    lax.fori_loop(0, live_blocks, add_block, 0)
+
+    def drain(k, carry):
         part(k).wait()
-    lax.fori_loop(0, live_blocks, add_block, 0)
+        return carry
+
+    lax.fori_loop(live_blocks, steps, drain, 0)
     for copy in whole[4:]:
         copy.wait()
     embed = embed_ref[...]
@@ -388,25 +417,17 @@
 
     edges = edge_slot.shape[0]
     mesh_count = mesh_features.shape[1]
-    step = min(512, edges)
+    step = min(EDGE_BLOCK, edges)
     steps = edges // step
     slots = edge_slot.reshape(1, edges)
     receivers = edge_receiver.reshape(1, edges)
-    smem = pl.BlockSpec(memory_space=pltpu.SMEM)
     lane_block = lambda i: (0, i)
 
-    square = jax.ShapeDtypeStruct((width, width), bf16)
-    pre, sender_t, message_t, node_t, output_t, mesh_embed = pl.pallas_call(
+    store = jax.ShapeDtypeStruct((4, width, 2 * width), bf16)
+    pre, kept = pl.pallas_call(
         functools.partial(early_kernel, far),
         grid=(steps,),
-        out_shape=(
-            jax.ShapeDtypeStruct((steps, width, step), bf16),
-            square,
-            square,
-            jax.ShapeDtypeStruct((width, 2 * width), bf16),
-            square,
-            jax.ShapeDtypeStruct((width, mesh_count), bf16),
-        ),
+        out_shape=(jax.ShapeDtypeStruct((steps, width, step), bf16), store),
         in_specs=[
             vmem(first_w.shape),
             vmem((edge_geometry.shape[0], step), lane_block),
@@ -416,11 +437,7 @@
         + [vmem(piece.shape) for piece in weights],
         out_specs=(
             vmem((1, width, step), lambda i: (i, 0, 0)),
-            vmem((width, width)),
-            vmem((width, width)),
-            vmem((width, 2 * width)),
-            vmem((width, width)),
-            vmem((width, mesh_count)),
+            vmem(store.shape),
         ),
         scratch_shapes=[
             pltpu.VMEM((width, width), bf16),
@@ -435,18 +452,36 @@
         name="early",
     )(first_w, edge_geometry, mesh_features, receivers, *weights)
 
+    return late_call(far, mesh_count, edge_count, film, slots, receivers, arrived, grid_w, pre, kept)
+
+
+def late_call(far, mesh_count, edge_count, film, slots, receivers, arrived, grid_w, pre, kept):
     in_vmem = pl.BlockSpec(memory_space=pltpu.VMEM)
-    operands = (arrived, grid_w, sender_t, pre, message_t, mesh_embed, node_t, output_t)
+    smem = pl.BlockSpec(memory_space=pltpu.SMEM)
+    picks = arrived.shape[0]
+    width = grid_w.shape[0]
+    steps = pre.shape[0]
+    edges = slots.shape[1]
+    held = (
+        arrived.shape,
+        grid_w.shape,
+        (width, width),
+        pre.shape,
+        (width, width),
+        (width, mesh_count),
+        (width, 2 * width),
+        (width, width),
+        (width, picks),
+    )
     return pl.pallas_call(
         functools.partial(late_kernel, far),
         out_shape=jax.ShapeDtypeStruct((mesh_count, width), bf16),
-        in_specs=[smem] + [in_vmem] * 3 + [pl.BlockSpec(memory_space=pl.ANY)] * len(operands),
+        in_specs=[smem] + [in_vmem] * 3 + [pl.BlockSpec(memory_space=pl.ANY)] * 4,
         out_specs=in_vmem,
-        scratch_shapes=[pltpu.VMEM(x.shape, x.dtype) for x in operands]
+        scratch_shapes=[pltpu.VMEM(shape, bf16) for shape in held]
         + [
-            pltpu.VMEM((width, picks), bf16),
             pltpu.VMEM((width, mesh_count), f32),
-            pltpu.SemaphoreType.DMA((len(operands) - 1,)),
+            pltpu.SemaphoreType.DMA((7,)),
             pltpu.SemaphoreType.DMA((steps,)),
         ],
         cost_estimate=pl.CostEstimate(
@@ -454,9 +489,9 @@
             bytes_accessed=2 * edges * width,
             transcendentals=edges * width,
         ),
-        compiler_params=pltpu.CompilerParams(vmem_limit_bytes=59 << 20),
+        compiler_params=pltpu.CompilerParams(vmem_limit_bytes=51 << 20),
         name="late",
-    )(edge_count, film, slots, receivers, *operands)
+    )(edge_count, film, slots, receivers, arrived, grid_w, pre, kept)
 
 
 def solution(mesh):

time: 181 us -> 176 us (0.972)
  Pallas kernels: 34.9 us -> 31.4 us
    pallas_call x1, Pallas kernels: 16.8 us -> 14.3 us  [late_call(): pl.pallas_call(functools.partial(late_kernel, far), out_shape=jax.ShapeDt...]
  transfers between devices with their start and end apart: 12 -> 12, of which waited for: 5 -> 6; matrix products, arithmetic and copies ran while one was open for 3% -> 2% of each run, Pallas kernels for 9% -> 9%
where the time goes in v1:
time: 176 us; the launch traced here: 173 us
  waiting for transfers between devices  89.1 us (51%)
  starting transfers between devices  46.8 us (27%)
  Pallas kernels  31.4 us (18%)
  local copies, waits for them, and re-layouts  2.7 us (2%)
  between operations  1.79 us (1%)
    ppermute x3, waiting for transfers between devices, gather_weights(): lax.ppermute(held, 'node', [(n, n ^ 2 * j) for n in range(nodes)])  49.9 us
    all_to_all x1, starting transfers between devices, gather_weights(): lax.all_to_all(held, 'node', 0, 0, tiled=True, axis_index_groups=strided)  31.7 us
    all_to_all x1, waiting for transfers between devices, gather_weights(): lax.all_to_all(held, 'node', 0, 0, tiled=True, axis_index_groups=strided)  21.9 us
    ppermute x3, waiting for transfers between devices, swap(): return lax.ppermute(values, ('member', 'node'), pairs)  16.7 us
    pallas_call x1, Pallas kernels, late_call(): pl.pallas_call(functools.partial(late_kernel, far), out_shape=jax.ShapeDt...  14.3 us
    pallas_call x1, Pallas kernels, per_device(): pl.pallas_call(functools.partial(early_kernel, far), grid=(steps,), out_s...  12.6 us
    all_to_all x1, starting transfers between devices, per_device(): lax.all_to_all(outgoing.reshape(nodes, picks // nodes, padded), 'node', 0...  7.39 us
    ppermute x3, starting transfers between devices, gather_weights(): lax.ppermute(held, 'node', [(n, n ^ 2 * j) for n in range(nodes)])  4.51 us
  transfers between devices with their start and end apart: 12, of which 6 were waited for; matrix products, arithmetic and copies ran while one was open for 2% of the time, Pallas kernels for 9%

profile of v1, /device:TPU:46, one launch (start us, length us, event | category | flops | bytes accessed | tf_op | source)
XLA Modules:
  0.0 173.1 jit_solution(17112971599154351988)
XLA Ops:
  0.0 0.0 copy-start
  0.0 1.5 pack.1
  1.5 0.0 copy-start.6
  1.5 0.0 copy-start.7
  1.5 31.7 %all-to-all-start.1 = ((bf16[8,56,128]{2,1,0:T(8,128)(2,1)}), bf16[8,56,128]{2,1,0:T(8,128)(2,1)S(1)}, u32[]{:S(2)}, u32[]{:S(2)}) async-start(bf16[8,56,128]{2,1,0:T(8,128)(2,1)} %pack.1), calls=%async_computation.1 | async-start | bytes 229376 | tf_op jit(solution)/shard_map/all_to_all | solution.py:321
  33.9 0.8 copy.31
  34.7 0.7 reshape.42.rows_ref
  35.4 0.6 pad_maximum_fusion.2.noise_ref
  36.0 0.0 copy-start.3
  36.0 3.0 %pick_rows.1 = bf16[1024,256]{1,0:T(8,128)(2,1)} custom-call(f32[2]{0:T(128)} %pad_maximum_fusion.2.noise_ref, bf16[168,1024]{1,0:T(8,128)(2,1)} %cond_ref.1, f32[84,1024]{1,0:T(8,128)} %target_ref.1, f32[84,1024]{1,0:T(8,128)} %sample_ref.1, s32[1,1024]{1,0:T(1,128)} %reshape.42.rows_ref), custom_call_target="tpu_custom_call" | custom-call | flops 536870912 | bytes 1048576 | tf_op jit(solution)/shard_map/pick_rows/pallas_call | solution.py:392
  39.0 21.9 %all-to-all-done.1 = bf16[8,56,128]{2,1,0:T(8,128)(2,1)S(1)} async-done(((bf16[8,56,128]{2,1,0:T(8,128)(2,1)}), bf16[8,56,128]{2,1,0:T(8,128)(2,1)S(1)}, u32[]{:S(2)}, u32[]{:S(2)}) %all-to-all-start.1) | async-done | bytes 114720 | tf_op jit(solution)/shard_map/all_to_all | solution.py:321
  60.9 7.4 %all-to-all-start = ((bf16[64,16,256]{2,1,0:T(8,128)(2,1)}), bf16[64,16,256]{2,1,0:T(8,128)(2,1)S(1)}, u32[]{:S(2)}, u32[]{:S(2)}) async-start(bf16[64,16,256]{2,1,0:T(8,128)(2,1)} %bitcast.34), calls=%async_computation | async-start | bytes 1048576 | tf_op jit(solution)/shard_map/all_to_all | solution.py:405
  68.3 0.0 copy-start.5
  68.3 1.2 collective-permute-start
  69.5 2.0 %collective-permute-start.1 = (bf16[8,56,128]{2,1,0:T(8,128)(2,1)S(1)}, bf16[8,56,128]{2,1,0:T(8,128)(2,1)S(1)}, u32[]{:S(2)}, u32[]{:S(2)}) collective-permute-start(bf16[8,56,128]{2,1,0:T(8,128)(2,1)S(1)} %all-to-all-done.1), channel_id=1, source_target_pairs={{0,4},{1,5},{2,6},{3,7},{4,0},{5,1},{6,2},{7,3},{8,12},{9,13},{10,... | collective-permute-start | bytes 344072 | tf_op jit(solution)/shard_map/ppermute | solution.py:323
  71.5 1.3 collective-permute-start.2
  72.8 45.4 %collective-permute-done = bf16[8,56,128]{2,1,0:T(8,128)(2,1)S(1)} collective-permute-done((bf16[8,56,128]{2,1,0:T(8,128)(2,1)S(1)}, bf16[8,56,128]{2,1,0:T(8,128)(2,1)S(1)}, u32[]{:S(2)}, u32[]{:S(2)}) %collective-permute-start) | collective-permute-done | bytes 114720 | tf_op jit(solution)/shard_map/ppermute | solution.py:323
  118.2 0.0 collective-permute-done.1
  118.2 4.5 %collective-permute-done.2 = bf16[8,56,128]{2,1,0:T(8,128)(2,1)S(1)} collective-permute-done((bf16[8,56,128]{2,1,0:T(8,128)(2,1)S(1)}, bf16[8,56,128]{2,1,0:T(8,128)(2,1)S(1)}, u32[]{:S(2)}, u32[]{:S(2)}) %collective-permute-start.2) | collective-permute-done | bytes 114720 | tf_op jit(solution)/shard_map/ppermute | solution.py:323
  122.7 0.1 pad_maximum_fusion.refs_0_
  122.8 0.0 copy-start.4
  122.8 0.0 copy-start.8
  122.8 0.5 collective-permute-start.3
  123.4 0.0 copy-done.6
  123.4 0.0 copy-done.7
  123.4 0.4 collective-permute-start.4
  123.8 11.3 %collective-permute-done.3.refs_1_ = bf16[4,8,56,128]{3,2,1,0:T(8,128)(2,1)} collective-permute-done((bf16[4,8,56,128]{3,2,1,0:T(8,128)(2,1)S(1)}, bf16[4,8,56,128]{3,2,1,0:T(8,128)(2,1)}, u32[]{:S(2)}, u32[]{:S(2)}) %collective-permute-start.3) | collective-permute-done | bytes 458784 | tf_op jit(solution)/shard_map/ppermute | solution.py:334
  135.1 1.5 collective-permute-start.5
  136.6 0.9 copy.33
  137.5 0.0 copy-done
  137.5 0.2 fusion.5
  137.7 0.1 collective-permute-start.6
  137.9 0.5 collective-permute-start.7
  138.3 0.0 collective-permute-done.4.refs_2_
  138.3 0.2 collective-permute-start.8
  138.5 5.4 %collective-permute-done.5.refs_3_ = bf16[4,8,56,128]{3,2,1,0:T(8,128)(2,1)} collective-permute-done((bf16[4,8,56,128]{3,2,1,0:T(8,128)(2,1)}, bf16[4,8,56,128]{3,2,1,0:T(8,128)(2,1)}, u32[]{:S(2)}, u32[]{:S(2)}) %collective-permute-start.5) | collective-permute-done | bytes 458784 | tf_op jit(solution)/shard_map/ppermute | solution.py:334
  143.9 0.0 collective-permute-start.9
  143.9 0.0 copy-done.3
  143.9 0.4 fusion
  144.2 0.2 copy.35
  144.4 0.0 copy-done.5
  144.4 0.1 copy.32
  145.3 0.0 copy-done.8
  145.3 0.0 copy-done.4
  145.3 0.0 collective-permute-done.6.refs_4_
  145.3 0.0 collective-permute-done.7.refs_5_
  145.3 0.0 collective-permute-done.8.refs_6_
  145.3 0.7 collective-permute-done.9.refs_7_
  146.0 0.0 copy-start.1
  146.0 0.0 copy-start.2
  146.0 12.6 %early.1 = (bf16[4,512,1024]{2,1,0:T(8,128)(2,1)}, bf16[4,512,1024]{2,1,0:T(8,128)(2,1)}) custom-call(f32[512,7]{1,0:T(8,128)} %bitcast.36, f32[4,4096]{1,0:T(4,128)} %geom_ref.1, f32[3,640]{1,0:T(4,128)} %mesh_ref.1, s32[1,4096]{1,0:T(1,128)} %bitcast.30, bf16[4,8,56,128]{3,2,1,0:T(8,128)(2,1)} %copy-done.4, ...), custom_call_target="tpu_custom_call" | custom-call | flops 5905580032 | bytes 18874368 | tf_op jit(solution)/shard_map/early/pallas_call | solution.py:427
  158.6 0.0 all-to-all-done
  158.6 0.0 copy-done.1
  158.6 0.0 copy-done.2
  158.6 14.3 %late.1 = bf16[640,512]{1,0:T(8,128)(2,1)} custom-call(s32[1]{0:T(128)S(6)} %copy.42.count_ref, f32[512,4]{1,0:T(8,128)S(1)} %fusion.3.film_ref, s32[1,4096]{1,0:T(1,128)S(1)} %bitcast.29, s32[1,4096]{1,0:T(1,128)S(1)} %bitcast.31, bf16[1024,256]{1,0:T(8,128)(2,1)S(1)} %bitcast.28, bf16[512,256]{1,0:T(8,128)(2,1)S(1)} %pad.4.grid_w_hbm, ...), custom_call_target="tpu_custom_call" | custom-call | flops 9126805504 | bytes 4194304 | tf_op jit(solution)/shard_map/late/pallas_call | solution.py:476
  (6 shorter events, 0.1 us)
Async XLA Ops:
  0.0 137.5 %copy-start = (f32[32,512]{1,0:T(8,128)S(1)}, f32[32,512]{1,0:T(8,128)}, u32[]{:S(2)}) copy-start(f32[32,512]{1,0:T(8,128)} %param.41) | copy-start | bytes 196612
  1.5 121.9 %copy-start.6 = (f32[3,512]{1,0:T(4,128)S(1)}, f32[3,512]{1,0:T(4,128)}, u32[]{:S(2)}) copy-start(f32[3,512]{1,0:T(4,128)} %param.33) | copy-start | bytes 18436
  1.5 121.9 %copy-start.7 = (f32[4,512]{1,0:T(4,128)S(1)}, f32[4,512]{1,0:T(4,128)}, u32[]{:S(2)}) copy-start(f32[4,512]{1,0:T(4,128)} %param.34) | copy-start | bytes 24580
  1.5 59.4 %all-to-all-start.1 = ((bf16[8,56,128]{2,1,0:T(8,128)(2,1)}), bf16[8,56,128]{2,1,0:T(8,128)(2,1)S(1)}, u32[]{:S(2)}, u32[]{:S(2)}) async-start(bf16[8,56,128]{2,1,0:T(8,128)(2,1)} %pack.1), calls=%async_computation.1 | async-start | bytes 229376 | tf_op jit(solution)/shard_map/all_to_all | solution.py:321
  36.0 107.9 %copy-start.3 = (bf16[512,2048]{1,0:T(8,128)(2,1)S(1)}, bf16[512,2048]{1,0:T(8,128)(2,1)}, u32[]{:S(2)}) copy-start(bf16[512,2048]{1,0:T(8,128)(2,1)} %param.42) | copy-start | bytes 6291460
  60.9 97.7 %all-to-all-start = ((bf16[64,16,256]{2,1,0:T(8,128)(2,1)}), bf16[64,16,256]{2,1,0:T(8,128)(2,1)S(1)}, u32[]{:S(2)}, u32[]{:S(2)}) async-start(bf16[64,16,256]{2,1,0:T(8,128)(2,1)} %bitcast.34), calls=%async_computation | async-start | bytes 1048576 | tf_op jit(solution)/shard_map/all_to_all | solution.py:405
  68.3 76.1 %copy-start.5 = (bf16[252,512]{1,0:T(8,128)(2,1)S(1)}, bf16[252,512]{1,0:T(8,128)(2,1)}, u32[]{:S(2)}) copy-start(bf16[252,512]{1,0:T(8,128)(2,1)} %param.32) | copy-start | bytes 774148
  68.3 49.9 %collective-permute-start = (bf16[8,56,128]{2,1,0:T(8,128)(2,1)S(1)}, bf16[8,56,128]{2,1,0:T(8,128)(2,1)S(1)}, u32[]{:S(2)}, u32[]{:S(2)}) collective-permute-start(bf16[8,56,128]{2,1,0:T(8,128)(2,1)S(1)} %all-to-all-done.1), channel_id=1, source_target_pairs={{0,2},{1,3},{2,0},{3,1},{4,6},{5,7},{6,4},{7,5},{8,10},{9,11},{10,... | collective-permute-start | bytes 344072 | tf_op jit(solution)/shard_map/ppermute | solution.py:323
  69.5 48.8 %collective-permute-start.1 = (bf16[8,56,128]{2,1,0:T(8,128)(2,1)S(1)}, bf16[8,56,128]{2,1,0:T(8,128)(2,1)S(1)}, u32[]{:S(2)}, u32[]{:S(2)}) collective-permute-start(bf16[8,56,128]{2,1,0:T(8,128)(2,1)S(1)} %all-to-all-done.1), channel_id=1, source_target_pairs={{0,4},{1,5},{2,6},{3,7},{4,0},{5,1},{6,2},{7,3},{8,12},{9,13},{10,... | collective-permute-start | bytes 344072 | tf_op jit(solution)/shard_map/ppermute | solution.py:323
  71.5 51.2 %collective-permute-start.2 = (bf16[8,56,128]{2,1,0:T(8,128)(2,1)S(1)}, bf16[8,56,128]{2,1,0:T(8,128)(2,1)S(1)}, u32[]{:S(2)}, u32[]{:S(2)}) collective-permute-start(bf16[8,56,128]{2,1,0:T(8,128)(2,1)S(1)} %all-to-all-done.1), channel_id=1, source_target_pairs={{0,6},{1,7},{2,4},{3,5},{4,2},{5,3},{6,0},{7,1},{8,14},{9,15},{10,... | collective-permute-start | bytes 344072 | tf_op jit(solution)/shard_map/ppermute | solution.py:323
  122.8 22.5 %copy-start.4 = (bf16[4,8,56,128]{3,2,1,0:T(8,128)(2,1)}, bf16[4,8,56,128]{3,2,1,0:T(8,128)(2,1)S(1)}, u32[]{:S(2)}) copy-start(bf16[4,8,56,128]{3,2,1,0:T(8,128)(2,1)S(1)} %pad_maximum_fusion.refs_0_) | copy-start | bytes 1376260
  122.8 22.5 %copy-start.8 = (f32[4]{0:T(128)S(1)}, f32[4]{0:T(128)}, u32[]{:S(2)}) copy-start(f32[4]{0:T(128)} %constant.28.clone) | copy-start | bytes 52
  122.8 12.3 %collective-permute-start.3 = (bf16[4,8,56,128]{3,2,1,0:T(8,128)(2,1)S(1)}, bf16[4,8,56,128]{3,2,1,0:T(8,128)(2,1)}, u32[]{:S(2)}, u32[]{:S(2)}) collective-permute-start(bf16[4,8,56,128]{3,2,1,0:T(8,128)(2,1)S(1)} %pad_maximum_fusion.refs_0_), channel_id=1, source_target_pairs={{0,64},{1,129},{2,66},{3,131},{4,68},{5,133},{6,70},{7,135},{8,72}... | collective-permute-start | bytes 1376264 | tf_op jit(solution)/shard_map/ppermute | solution.py:334
  123.4 14.9 %collective-permute-start.4 = (bf16[4,8,56,128]{3,2,1,0:T(8,128)(2,1)S(1)}, bf16[4,8,56,128]{3,2,1,0:T(8,128)(2,1)}, u32[]{:S(2)}, u32[]{:S(2)}) collective-permute-start(bf16[4,8,56,128]{3,2,1,0:T(8,128)(2,1)S(1)} %pad_maximum_fusion.refs_0_), channel_id=1, source_target_pairs={{0,128},{1,65},{2,130},{3,67},{4,132},{5,69},{6,134},{7,71},{8,136... | collective-permute-start | bytes 1376264 | tf_op jit(solution)/shard_map/ppermute | solution.py:334
  135.1 8.8 %collective-permute-start.5 = (bf16[4,8,56,128]{3,2,1,0:T(8,128)(2,1)}, bf16[4,8,56,128]{3,2,1,0:T(8,128)(2,1)}, u32[]{:S(2)}, u32[]{:S(2)}) collective-permute-start(bf16[4,8,56,128]{3,2,1,0:T(8,128)(2,1)} %collective-permute-done.3.refs_1_), channel_id=1, source_target_pairs={{0,128},{1,65},{2,130},{3,67},{4,132},{5,69},{6,134},{7,71},{8,136... | collective-permute-start | bytes 1376264 | tf_op jit(solution)/shard_map/ppermute | solution.py:334
  137.7 7.6 %collective-permute-start.6 = (bf16[4,8,56,128]{3,2,1,0:T(8,128)(2,1)S(1)}, bf16[4,8,56,128]{3,2,1,0:T(8,128)(2,1)}, u32[]{:S(2)}, u32[]{:S(2)}) collective-permute-start(bf16[4,8,56,128]{3,2,1,0:T(8,128)(2,1)S(1)} %pad_maximum_fusion.refs_0_), channel_id=1, source_target_pairs={{0,1},{1,0},{2,3},{3,2},{4,5},{5,4},{6,7},{7,6},{8,9},{9,8},{10,11... | collective-permute-start | bytes 1376264 | tf_op jit(solution)/shard_map/ppermute | solution.py:341
  137.9 7.5 %collective-permute-start.7 = (bf16[4,8,56,128]{3,2,1,0:T(8,128)(2,1)}, bf16[4,8,56,128]{3,2,1,0:T(8,128)(2,1)}, u32[]{:S(2)}, u32[]{:S(2)}) collective-permute-start(bf16[4,8,56,128]{3,2,1,0:T(8,128)(2,1)} %collective-permute-done.3.refs_1_), channel_id=1, source_target_pairs={{0,1},{1,0},{2,3},{3,2},{4,5},{5,4},{6,7},{7,6},{8,9},{9,8},{10,11... | collective-permute-start | bytes 1376264 | tf_op jit(solution)/shard_map/ppermute | solution.py:341
  138.3 7.0 %collective-permute-start.8 = (bf16[4,8,56,128]{3,2,1,0:T(8,128)(2,1)}, bf16[4,8,56,128]{3,2,1,0:T(8,128)(2,1)}, u32[]{:S(2)}, u32[]{:S(2)}) collective-permute-start(bf16[4,8,56,128]{3,2,1,0:T(8,128)(2,1)} %collective-permute-done.4.refs_2_), channel_id=1, source_target_pairs={{0,1},{1,0},{2,3},{3,2},{4,5},{5,4},{6,7},{7,6},{8,9},{9,8},{10,11... | collective-permute-start | bytes 1376264 | tf_op jit(solution)/shard_map/ppermute | solution.py:341
  143.9 2.2 %collective-permute-start.9 = (bf16[4,8,56,128]{3,2,1,0:T(8,128)(2,1)}, bf16[4,8,56,128]{3,2,1,0:T(8,128)(2,1)}, u32[]{:S(2)}, u32[]{:S(2)}) collective-permute-start(bf16[4,8,56,128]{3,2,1,0:T(8,128)(2,1)} %collective-permute-done.5.refs_3_), channel_id=1, source_target_pairs={{0,1},{1,0},{2,3},{3,2},{4,5},{5,4},{6,7},{7,6},{8,9},{9,8},{10,11... | collective-permute-start | bytes 1376264 | tf_op jit(solution)/shard_map/ppermute | solution.py:341
  146.0 12.6 %copy-start.1 = (s32[4096]{0:T(1024)S(1)}, s32[4096]{0:T(1024)}, u32[]{:S(2)}) copy-start(s32[4096]{0:T(1024)} %param.28) | copy-start | bytes 49156
  146.0 12.6 %copy-start.2 = (s32[4096]{0:T(1024)S(1)}, s32[4096]{0:T(1024)}, u32[]{:S(2)}) copy-start(s32[4096]{0:T(1024)} %param.29) | copy-start | bytes 49156

commit v2 on v1

--- a/solution.py
+++ b/solution.py
@@ -145,7 +145,8 @@
             mask = (0, 1 + c, 2 - c, 3)[number % 4]
             q = quarter ^ mask
             piece = jnp.concatenate(
-                [piece_ref[chip ^ near].astype(f32) for near in range(NEAR)], axis=0
+                [piece_ref[(near - chip) & (NEAR - 1)].astype(f32) for near in range(NEAR)],
+                axis=0,
             )
             cols = pl.ds(pl.multiple_of(c * depth, depth), depth)
             wide = pl.ds(pl.multiple_of(c * 2 * depth, 2 * depth), 2 * depth)
@@ -320,8 +321,12 @@
     )(*blocks)
     held = lax.all_to_all(held, "node", 0, 0, tiled=True, axis_index_groups=strided)
     near = [
-        lax.ppermute(held, "node", [(n, n ^ (2 * j)) for n in range(nodes)])
-        for j in range(1, NEAR)
+        lax.ppermute(
+            held,
+            "node",
+            [((n + 2 * (odd if n % 2 else even)) % nodes, n) for n in range(nodes)],
+        )
+        for even, odd in ((1, 1), (2, -2), (-1, -1))
     ]
     held = jnp.stack([held] + near)
 

time: 176 us -> 172 us (0.977); the launches traced: 173 us -> 171 us
  waiting for transfers between devices: 89.1 us -> 87.2 us
    ppermute x3, waiting for transfers between devices: 49.9 us -> 45.2 us  [gather_weights(): lax.ppermute(held, 'node', [((n + 2 * (odd if n % 2 else even)) % nodes,...]
    ppermute x3, waiting for transfers between devices: 16.7 us -> 19.4 us  [swap(): return lax.ppermute(values, ('member', 'node'), pairs)]
  transfers between devices with their start and end apart: 12 -> 12, of which waited for: 6 -> 7; matrix products, arithmetic and copies ran while one was open for 2% -> 2% of each run, Pallas kernels for 9% -> 9%
where the time goes in v2:
time: 172 us; the launch traced here: 171 us
  waiting for transfers between devices  87.2 us (51%)
  starting transfers between devices  46.5 us (27%)
  Pallas kernels  31.4 us (18%)
  local copies, waits for them, and re-layouts  2.7 us (2%)
  between operations  1.79 us (1%)
    ppermute x3, waiting for transfers between devices, gather_weights(): lax.ppermute(held, 'node', [((n + 2 * (odd if n % 2 else even)) % nodes,...  45.2 us
    all_to_all x1, starting transfers between devices, gather_weights(): lax.all_to_all(held, 'node', 0, 0, tiled=True, axis_index_groups=strided)  31.7 us
    all_to_all x1, waiting for transfers between devices, gather_weights(): lax.all_to_all(held, 'node', 0, 0, tiled=True, axis_index_groups=strided)  21.9 us
    ppermute x3, waiting for transfers between devices, swap(): return lax.ppermute(values, ('member', 'node'), pairs)  19.4 us
    pallas_call x1, Pallas kernels, late_call(): pl.pallas_call(functools.partial(late_kernel, far), out_shape=jax.ShapeDt...  14.3 us
    pallas_call x1, Pallas kernels, per_device(): pl.pallas_call(functools.partial(early_kernel, far), grid=(steps,), out_s...  12.6 us
    all_to_all x1, starting transfers between devices, per_device(): lax.all_to_all(outgoing.reshape(nodes, picks // nodes, padded), 'node', 0...  7.39 us
    ppermute x3, starting transfers between devices, gather_weights(): lax.ppermute(held, 'node', [((n + 2 * (odd if n % 2 else even)) % nodes,...  5.77 us
  transfers between devices with their start and end apart: 12, of which 7 were waited for; matrix products, arithmetic and copies ran while one was open for 2% of the time, Pallas kernels for 9%

profile of v2, /device:TPU:46, one launch (start us, length us, event | category | flops | bytes accessed | tf_op | source)
XLA Modules:
  0.0 170.9 jit_solution(12264843646926508576)
XLA Ops:
  0.0 0.0 copy-start
  0.0 1.5 pack.1
  1.5 0.0 copy-start.6
  1.5 0.0 copy-start.7
  1.5 31.7 %all-to-all-start.1 = ((bf16[8,56,128]{2,1,0:T(8,128)(2,1)}), bf16[8,56,128]{2,1,0:T(8,128)(2,1)S(1)}, u32[]{:S(2)}, u32[]{:S(2)}) async-start(bf16[8,56,128]{2,1,0:T(8,128)(2,1)} %pack.1), calls=%async_computation.1 | async-start | bytes 229376 | tf_op jit(solution)/shard_map/all_to_all | solution.py:322
  33.9 0.8 copy.31
  34.7 0.7 reshape.42.rows_ref
  35.4 0.6 pad_maximum_fusion.2.noise_ref
  36.0 0.0 copy-start.3
  36.0 3.0 %pick_rows.1 = bf16[1024,256]{1,0:T(8,128)(2,1)} custom-call(f32[2]{0:T(128)} %pad_maximum_fusion.2.noise_ref, bf16[168,1024]{1,0:T(8,128)(2,1)} %cond_ref.1, f32[84,1024]{1,0:T(8,128)} %target_ref.1, f32[84,1024]{1,0:T(8,128)} %sample_ref.1, s32[1,1024]{1,0:T(1,128)} %reshape.42.rows_ref), custom_call_target="tpu_custom_call" | custom-call | flops 536870912 | bytes 1048576 | tf_op jit(solution)/shard_map/pick_rows/pallas_call | solution.py:397
  39.0 21.9 %all-to-all-done.1 = bf16[8,56,128]{2,1,0:T(8,128)(2,1)S(1)} async-done(((bf16[8,56,128]{2,1,0:T(8,128)(2,1)}), bf16[8,56,128]{2,1,0:T(8,128)(2,1)S(1)}, u32[]{:S(2)}, u32[]{:S(2)}) %all-to-all-start.1) | async-done | bytes 114720 | tf_op jit(solution)/shard_map/all_to_all | solution.py:322
  60.9 7.4 %all-to-all-start = ((bf16[64,16,256]{2,1,0:T(8,128)(2,1)}), bf16[64,16,256]{2,1,0:T(8,128)(2,1)S(1)}, u32[]{:S(2)}, u32[]{:S(2)}) async-start(bf16[64,16,256]{2,1,0:T(8,128)(2,1)} %bitcast.34), calls=%async_computation | async-start | bytes 1048576 | tf_op jit(solution)/shard_map/all_to_all | solution.py:410
  68.3 0.0 copy-start.5
  68.3 2.9 %collective-permute-start = (bf16[8,56,128]{2,1,0:T(8,128)(2,1)S(1)}, bf16[8,56,128]{2,1,0:T(8,128)(2,1)S(1)}, u32[]{:S(2)}, u32[]{:S(2)}) collective-permute-start(bf16[8,56,128]{2,1,0:T(8,128)(2,1)S(1)} %all-to-all-done.1), channel_id=1, source_target_pairs={{2,0},{3,1},{4,2},{5,3},{6,4},{7,5},{8,6},{9,7},{10,8},{11,9},{12,... | collective-permute-start | bytes 344072 | tf_op jit(solution)/shard_map/ppermute | solution.py:324
  71.2 2.3 %collective-permute-start.1 = (bf16[8,56,128]{2,1,0:T(8,128)(2,1)S(1)}, bf16[8,56,128]{2,1,0:T(8,128)(2,1)S(1)}, u32[]{:S(2)}, u32[]{:S(2)}) collective-permute-start(bf16[8,56,128]{2,1,0:T(8,128)(2,1)S(1)} %all-to-all-done.1), channel_id=1, source_target_pairs={{4,0},{61,1},{6,2},{63,3},{8,4},{1,5},{10,6},{3,7},{12,8},{5,9},{1... | collective-permute-start | bytes 344072 | tf_op jit(solution)/shard_map/ppermute | solution.py:324
  73.5 0.6 collective-permute-start.2
  74.1 40.9 %collective-permute-done = bf16[8,56,128]{2,1,0:T(8,128)(2,1)S(1)} collective-permute-done((bf16[8,56,128]{2,1,0:T(8,128)(2,1)S(1)}, bf16[8,56,128]{2,1,0:T(8,128)(2,1)S(1)}, u32[]{:S(2)}, u32[]{:S(2)}) %collective-permute-start) | collective-permute-done | bytes 114720 | tf_op jit(solution)/shard_map/ppermute | solution.py:324
  115.0 4.2 %collective-permute-done.1 = bf16[8,56,128]{2,1,0:T(8,128)(2,1)S(1)} collective-permute-done((bf16[8,56,128]{2,1,0:T(8,128)(2,1)S(1)}, bf16[8,56,128]{2,1,0:T(8,128)(2,1)S(1)}, u32[]{:S(2)}, u32[]{:S(2)}) %collective-permute-start.1) | collective-permute-done | bytes 114720 | tf_op jit(solution)/shard_map/ppermute | solution.py:324
  119.2 0.1 collective-permute-done.2
  119.3 0.1 pad_maximum_fusion.refs_0_
  119.3 0.0 copy-start.4
  119.3 0.0 copy-start.8
  119.3 0.5 collective-permute-start.3
  119.9 0.0 copy-done.6
  119.9 0.0 copy-done.7
  120.0 0.4 collective-permute-start.4
  120.3 12.6 %collective-permute-done.3.refs_1_ = bf16[4,8,56,128]{3,2,1,0:T(8,128)(2,1)} collective-permute-done((bf16[4,8,56,128]{3,2,1,0:T(8,128)(2,1)S(1)}, bf16[4,8,56,128]{3,2,1,0:T(8,128)(2,1)}, u32[]{:S(2)}, u32[]{:S(2)}) %collective-permute-start.3) | collective-permute-done | bytes 458784 | tf_op jit(solution)/shard_map/ppermute | solution.py:339
  132.9 0.0 collective-permute-start.5
  132.9 0.9 copy.33
  133.8 0.0 copy-done
  133.8 0.2 fusion.5
  134.0 0.1 collective-permute-start.6
  134.2 0.5 collective-permute-start.7
  134.7 0.0 collective-permute-done.4.refs_2_
  134.7 0.2 collective-permute-start.8
  134.8 6.8 %collective-permute-done.5.refs_3_ = bf16[4,8,56,128]{3,2,1,0:T(8,128)(2,1)} collective-permute-done((bf16[4,8,56,128]{3,2,1,0:T(8,128)(2,1)}, bf16[4,8,56,128]{3,2,1,0:T(8,128)(2,1)}, u32[]{:S(2)}, u32[]{:S(2)}) %collective-permute-start.5) | collective-permute-done | bytes 458784 | tf_op jit(solution)/shard_map/ppermute | solution.py:339
  141.7 0.0 collective-permute-start.9
  141.7 0.0 copy-done.3
  141.7 0.4 fusion
  142.0 0.2 copy.35
  142.2 0.0 copy-done.5
  142.2 0.1 copy.32
  143.1 0.0 copy-done.8
  143.1 0.0 copy-done.4
  143.1 0.0 collective-permute-done.6.refs_4_
  143.1 0.0 collective-permute-done.7.refs_5_
  143.1 0.0 collective-permute-done.8.refs_6_
  143.1 0.7 collective-permute-done.9.refs_7_
  143.8 0.0 copy-start.1
  143.8 0.0 copy-start.2
  143.8 12.6 %early.1 = (bf16[4,512,1024]{2,1,0:T(8,128)(2,1)}, bf16[4,512,1024]{2,1,0:T(8,128)(2,1)}) custom-call(f32[512,7]{1,0:T(8,128)} %bitcast.36, f32[4,4096]{1,0:T(4,128)} %geom_ref.1, f32[3,640]{1,0:T(4,128)} %mesh_ref.1, s32[1,4096]{1,0:T(1,128)} %bitcast.30, bf16[4,8,56,128]{3,2,1,0:T(8,128)(2,1)} %copy-done.4, ...), custom_call_target="tpu_custom_call" | custom-call | flops 5905580032 | bytes 18874368 | tf_op jit(solution)/shard_map/early/pallas_call | solution.py:432
  156.4 0.0 all-to-all-done
  156.4 0.0 copy-done.1
  156.4 0.0 copy-done.2
  156.4 14.3 %late.1 = bf16[640,512]{1,0:T(8,128)(2,1)} custom-call(s32[1]{0:T(128)S(6)} %copy.42.count_ref, f32[512,4]{1,0:T(8,128)S(1)} %fusion.3.film_ref, s32[1,4096]{1,0:T(1,128)S(1)} %bitcast.29, s32[1,4096]{1,0:T(1,128)S(1)} %bitcast.31, bf16[1024,256]{1,0:T(8,128)(2,1)S(1)} %bitcast.28, bf16[512,256]{1,0:T(8,128)(2,1)S(1)} %pad.4.grid_w_hbm, ...), custom_call_target="tpu_custom_call" | custom-call | flops 9126805504 | bytes 4194304 | tf_op jit(solution)/shard_map/late/pallas_call | solution.py:481
  (6 shorter events, 0.1 us)
Async XLA Ops:
  0.0 133.8 %copy-start = (f32[32,512]{1,0:T(8,128)S(1)}, f32[32,512]{1,0:T(8,128)}, u32[]{:S(2)}) copy-start(f32[32,512]{1,0:T(8,128)} %param.41) | copy-start | bytes 196612
  1.5 118.4 %copy-start.6 = (f32[3,512]{1,0:T(4,128)S(1)}, f32[3,512]{1,0:T(4,128)}, u32[]{:S(2)}) copy-start(f32[3,512]{1,0:T(4,128)} %param.33) | copy-start | bytes 18436
  1.5 118.4 %copy-start.7 = (f32[4,512]{1,0:T(4,128)S(1)}, f32[4,512]{1,0:T(4,128)}, u32[]{:S(2)}) copy-start(f32[4,512]{1,0:T(4,128)} %param.34) | copy-start | bytes 24580
  1.5 59.4 %all-to-all-start.1 = ((bf16[8,56,128]{2,1,0:T(8,128)(2,1)}), bf16[8,56,128]{2,1,0:T(8,128)(2,1)S(1)}, u32[]{:S(2)}, u32[]{:S(2)}) async-start(bf16[8,56,128]{2,1,0:T(8,128)(2,1)} %pack.1), calls=%async_computation.1 | async-start | bytes 229376 | tf_op jit(solution)/shard_map/all_to_all | solution.py:322
  36.0 105.7 %copy-start.3 = (bf16[512,2048]{1,0:T(8,128)(2,1)S(1)}, bf16[512,2048]{1,0:T(8,128)(2,1)}, u32[]{:S(2)}) copy-start(bf16[512,2048]{1,0:T(8,128)(2,1)} %param.42) | copy-start | bytes 6291460
  60.9 95.5 %all-to-all-start = ((bf16[64,16,256]{2,1,0:T(8,128)(2,1)}), bf16[64,16,256]{2,1,0:T(8,128)(2,1)S(1)}, u32[]{:S(2)}, u32[]{:S(2)}) async-start(bf16[64,16,256]{2,1,0:T(8,128)(2,1)} %bitcast.34), calls=%async_computation | async-start | bytes 1048576 | tf_op jit(solution)/shard_map/all_to_all | solution.py:410
  68.3 73.9 %copy-start.5 = (bf16[252,512]{1,0:T(8,128)(2,1)S(1)}, bf16[252,512]{1,0:T(8,128)(2,1)}, u32[]{:S(2)}) copy-start(bf16[252,512]{1,0:T(8,128)(2,1)} %param.32) | copy-start | bytes 774148
  68.3 46.7 %collective-permute-start = (bf16[8,56,128]{2,1,0:T(8,128)(2,1)S(1)}, bf16[8,56,128]{2,1,0:T(8,128)(2,1)S(1)}, u32[]{:S(2)}, u32[]{:S(2)}) collective-permute-start(bf16[8,56,128]{2,1,0:T(8,128)(2,1)S(1)} %all-to-all-done.1), channel_id=1, source_target_pairs={{2,0},{3,1},{4,2},{5,3},{6,4},{7,5},{8,6},{9,7},{10,8},{11,9},{12,... | collective-permute-start | bytes 344072 | tf_op jit(solution)/shard_map/ppermute | solution.py:324
  71.2 48.0 %collective-permute-start.1 = (bf16[8,56,128]{2,1,0:T(8,128)(2,1)S(1)}, bf16[8,56,128]{2,1,0:T(8,128)(2,1)S(1)}, u32[]{:S(2)}, u32[]{:S(2)}) collective-permute-start(bf16[8,56,128]{2,1,0:T(8,128)(2,1)S(1)} %all-to-all-done.1), channel_id=1, source_target_pairs={{4,0},{61,1},{6,2},{63,3},{8,4},{1,5},{10,6},{3,7},{12,8},{5,9},{1... | collective-permute-start | bytes 344072 | tf_op jit(solution)/shard_map/ppermute | solution.py:324
  73.5 45.8 %collective-permute-start.2 = (bf16[8,56,128]{2,1,0:T(8,128)(2,1)S(1)}, bf16[8,56,128]{2,1,0:T(8,128)(2,1)S(1)}, u32[]{:S(2)}, u32[]{:S(2)}) collective-permute-start(bf16[8,56,128]{2,1,0:T(8,128)(2,1)S(1)} %all-to-all-done.1), channel_id=1, source_target_pairs={{62,0},{63,1},{0,2},{1,3},{2,4},{3,5},{4,6},{5,7},{6,8},{7,9},{8,1... | collective-permute-start | bytes 344072 | tf_op jit(solution)/shard_map/ppermute | solution.py:324
  119.3 23.8 %copy-start.4 = (bf16[4,8,56,128]{3,2,1,0:T(8,128)(2,1)}, bf16[4,8,56,128]{3,2,1,0:T(8,128)(2,1)S(1)}, u32[]{:S(2)}) copy-start(bf16[4,8,56,128]{3,2,1,0:T(8,128)(2,1)S(1)} %pad_maximum_fusion.refs_0_) | copy-start | bytes 1376260
  119.3 23.7 %copy-start.8 = (f32[4]{0:T(128)S(1)}, f32[4]{0:T(128)}, u32[]{:S(2)}) copy-start(f32[4]{0:T(128)} %constant.28.clone) | copy-start | bytes 52
  119.3 13.5 %collective-permute-start.3 = (bf16[4,8,56,128]{3,2,1,0:T(8,128)(2,1)S(1)}, bf16[4,8,56,128]{3,2,1,0:T(8,128)(2,1)}, u32[]{:S(2)}, u32[]{:S(2)}) collective-permute-start(bf16[4,8,56,128]{3,2,1,0:T(8,128)(2,1)S(1)} %pad_maximum_fusion.refs_0_), channel_id=1, source_target_pairs={{0,64},{1,129},{2,66},{3,131},{4,68},{5,133},{6,70},{7,135},{8,72}... | collective-permute-start | bytes 1376264 | tf_op jit(solution)/shard_map/ppermute | solution.py:339
  120.0 14.7 %collective-permute-start.4 = (bf16[4,8,56,128]{3,2,1,0:T(8,128)(2,1)S(1)}, bf16[4,8,56,128]{3,2,1,0:T(8,128)(2,1)}, u32[]{:S(2)}, u32[]{:S(2)}) collective-permute-start(bf16[4,8,56,128]{3,2,1,0:T(8,128)(2,1)S(1)} %pad_maximum_fusion.refs_0_), channel_id=1, source_target_pairs={{0,128},{1,65},{2,130},{3,67},{4,132},{5,69},{6,134},{7,71},{8,136... | collective-permute-start | bytes 1376264 | tf_op jit(solution)/shard_map/ppermute | solution.py:339
  132.9 8.8 %collective-permute-start.5 = (bf16[4,8,56,128]{3,2,1,0:T(8,128)(2,1)}, bf16[4,8,56,128]{3,2,1,0:T(8,128)(2,1)}, u32[]{:S(2)}, u32[]{:S(2)}) collective-permute-start(bf16[4,8,56,128]{3,2,1,0:T(8,128)(2,1)} %collective-permute-done.3.refs_1_), channel_id=1, source_target_pairs={{0,128},{1,65},{2,130},{3,67},{4,132},{5,69},{6,134},{7,71},{8,136... | collective-permute-start | bytes 1376264 | tf_op jit(solution)/shard_map/ppermute | solution.py:339
  134.0 9.1 %collective-permute-start.6 = (bf16[4,8,56,128]{3,2,1,0:T(8,128)(2,1)S(1)}, bf16[4,8,56,128]{3,2,1,0:T(8,128)(2,1)}, u32[]{:S(2)}, u32[]{:S(2)}) collective-permute-start(bf16[4,8,56,128]{3,2,1,0:T(8,128)(2,1)S(1)} %pad_maximum_fusion.refs_0_), channel_id=1, source_target_pairs={{0,1},{1,0},{2,3},{3,2},{4,5},{5,4},{6,7},{7,6},{8,9},{9,8},{10,11... | collective-permute-start | bytes 1376264 | tf_op jit(solution)/shard_map/ppermute | solution.py:346
  134.2 8.9 %collective-permute-start.7 = (bf16[4,8,56,128]{3,2,1,0:T(8,128)(2,1)}, bf16[4,8,56,128]{3,2,1,0:T(8,128)(2,1)}, u32[]{:S(2)}, u32[]{:S(2)}) collective-permute-start(bf16[4,8,56,128]{3,2,1,0:T(8,128)(2,1)} %collective-permute-done.3.refs_1_), channel_id=1, source_target_pairs={{0,1},{1,0},{2,3},{3,2},{4,5},{5,4},{6,7},{7,6},{8,9},{9,8},{10,11... | collective-permute-start | bytes 1376264 | tf_op jit(solution)/shard_map/ppermute | solution.py:346
  134.7 8.5 %collective-permute-start.8 = (bf16[4,8,56,128]{3,2,1,0:T(8,128)(2,1)}, bf16[4,8,56,128]{3,2,1,0:T(8,128)(2,1)}, u32[]{:S(2)}, u32[]{:S(2)}) collective-permute-start(bf16[4,8,56,128]{3,2,1,0:T(8,128)(2,1)} %collective-permute-done.4.refs_2_), channel_id=1, source_target_pairs={{0,1},{1,0},{2,3},{3,2},{4,5},{5,4},{6,7},{7,6},{8,9},{9,8},{10,11... | collective-permute-start | bytes 1376264 | tf_op jit(solution)/shard_map/ppermute | solution.py:346
  141.7 2.2 %collective-permute-start.9 = (bf16[4,8,56,128]{3,2,1,0:T(8,128)(2,1)}, bf16[4,8,56,128]{3,2,1,0:T(8,128)(2,1)}, u32[]{:S(2)}, u32[]{:S(2)}) collective-permute-start(bf16[4,8,56,128]{3,2,1,0:T(8,128)(2,1)} %collective-permute-done.5.refs_3_), channel_id=1, source_target_pairs={{0,1},{1,0},{2,3},{3,2},{4,5},{5,4},{6,7},{7,6},{8,9},{9,8},{10,11... | collective-permute-start | bytes 1376264 | tf_op jit(solution)/shard_map/ppermute | solution.py:346
  143.8 12.6 %copy-start.1 = (s32[4096]{0:T(1024)S(1)}, s32[4096]{0:T(1024)}, u32[]{:S(2)}) copy-start(s32[4096]{0:T(1024)} %param.28) | copy-start | bytes 49156
  143.8 12.6 %copy-start.2 = (s32[4096]{0:T(1024)S(1)}, s32[4096]{0:T(1024)}, u32[]{:S(2)}) copy-start(s32[4096]{0:T(1024)} %param.29) | copy-start | bytes 49156
